TPU v7x, 32 devices: a whole 2x2x4 slice. The times are simulated.
32 devices in a mesh: dp: 4 (over y, x), tp: 8 (over z, core).
Axes of the slice: x: 2, y: 2, z: 4, core: 2. Of those that a mesh axis runs over, the one named last changes fastest.
Arguments:
- gradients: bfloat16 [4, 4, 3072, 768], P('dp', None, 'tp'), may hold values from -6 to 6, as said below
- right_factor: float32 [4, 768, 8], replicated, may hold values from -6 to 6
- weights_before: float32 [4, 3072, 768], P(None, 'tp', 'dp'), may hold values from -0.21875 to 0.21875
- momentum: float32 [4, 3072, 768], P(None, 'tp', 'dp'), may hold values from -0.3125 to 0.3125
Outputs:
- new_weights: float32 [4, 3072, 768], P(None, 'tp', 'dp')
- new_basis: float32 [4, 768, 8], replicated
- new_momentum: float32 [4, 3072, 768], P(None, 'tp', 'dp')
Inputs may be any that keep to these rules, and one draw needn't show every extreme that they name: gradients holds numbers from -6 to 6.
All inputs are finite; a program needn't handle non-finite values.
Results may differ from a plain program's by a relative error of at most 0.0003.
Values sent between devices are 32-bit elements.
A program may use at most 64 MiB of HBM per device.

v0:
```python
import jax
import jax.numpy as jnp
from jax import lax
from jax.sharding import PartitionSpec as P

RANK = 8


def on_device(gradients, right_factor, weights_before, momentum):
    own_grads = gradients[0]
    part_left = jnp.einsum(
        "liw,lwr->lir",
        own_grads,
        right_factor.astype(jnp.bfloat16),
        preferred_element_type=jnp.float32,
    )
    left = lax.psum(part_left, "dp")
    part_gram = jnp.einsum("lir,lis->lrs", left, left, precision=lax.Precision.HIGHEST)
    small_left = left.astype(jnp.bfloat16)
    part_right = jnp.einsum(
        "liw,lir->lwr", own_grads, small_left, preferred_element_type=jnp.float32
    )
    own_share = part_gram / lax.axis_size("dp")
    right, gram = lax.psum((part_right, own_share), ("dp", "tp"))
    gram = gram + 0.001 * jnp.mean(jnp.diagonal(gram, axis1=1, axis2=2), axis=1)[
        :, None, None
    ] * jnp.eye(RANK, dtype=jnp.float32)
    place = lax.axis_index("dp") * weights_before.shape[2]
    own_right = lax.dynamic_slice_in_dim(right, place, weights_before.shape[2], axis=1)
    root = jnp.linalg.cholesky(gram)
    half = lax.linalg.triangular_solve(
        root, jnp.swapaxes(own_right, 1, 2), left_side=True, lower=True
    )
    mixed = lax.linalg.triangular_solve(root, half, left_side=True, lower=True, transpose_a=True)
    change = jnp.einsum(
        "lir,lrw->liw", left, mixed, precision=lax.Precision.HIGHEST
    ) / lax.axis_size("dp")
    new_momentum = 0.9 * momentum + change
    new_weights = weights_before - 0.02 * new_momentum
    new_basis = right * lax.rsqrt(jnp.mean(right * right, axis=(1, 2), keepdims=True) + 1e-12)
    return (new_weights, new_basis, new_momentum)


def solution(mesh):
    in_specs = (P("dp", None, "tp", None), P(), P(None, "tp", "dp"), P(None, "tp", "dp"))
    out_specs = (P(None, "tp", "dp"), P(), P(None, "tp", "dp"))
    return jax.shard_map(
        on_device, mesh=mesh, in_specs=in_specs, out_specs=out_specs, check_vma=False
    )
```

profile of v0, /device:TPU:8, one launch (start us, length us, event | category | flops | bytes accessed | tf_op | source)
XLA Modules:
  0.0 166.5 jit_solution(5481928536512770521)
XLA Ops:
  7.2 0.0 copy-start
  7.2 0.0 all-reduce.2.cloned.1.call-start
  7.2 1.6 copy-done
  8.8 1.6 fusion.2
  10.4 16.7 %psum.21 = f32[4,384,8]{1,2,0:T(8,128)S(1)} all-reduce(f32[4,384,8]{1,2,0:T(8,128)S(1)} %fusion.2), channel_id=1, replica_groups=mesh['dp'=4,'tp'=8] {'dp'}, use_global_device_ids=true, to_apply=%region_0.0 | all-reduce | flops 12288 | bytes 98304 | tf_op jit(solution)/shard_map/psum | solution.py:17
  27.1 1.1 fusion.5
  28.2 0.0 all-reduce.2.cloned.1.call-update
  28.3 0.2 convolution_multiply_fusion.1
  28.5 0.1 copy.13
  28.5 39.5 %psum.22 = f32[4,8,8]{1,2,0:T(8,128)S(1)} all-reduce(f32[4,8,8]{1,2,0:T(8,128)S(1)} %convolution_multiply_fusion.1), channel_id=1, replica_groups=mesh['dp'=4,'tp'=8] {'dp','tp'}, use_global_device_ids=true, to_apply=%region_1.0 | all-reduce | flops 256 | bytes 2048 | tf_op jit(solution)/shard_map/psum | solution.py:24
  68.0 0.1 copy.12
  68.1 0.6 gather_fusion
  68.7 0.1 multiply_add_fusion
  68.8 0.1 copy.14
  68.9 0.1 fusion.15
  69.0 2.9 %custom-call.9 = f32[4,8,8]{2,1,0:T(8,128)S(1)} custom-call(f32[4,8,8]{2,1,0:T(8,128)S(1)} %fusion.15), custom_call_target="Cholesky" | custom-call | tf_op jit(solution)/shard_map/jit(cholesky)/cholesky | solution.py:30
  71.9 0.1 select_reduce_fusion
  71.9 0.1 compare_reduce_fusion
  72.0 0.1 select_bitcast_fusion
  72.1 2.5 %custom-call.10 = f32[4,1,8,8]{2,3,1,0:T(8,128)S(1)} custom-call(f32[4,1,8,8]{3,2,1,0:T(8,128)S(1)} %select_bitcast_fusion), custom_call_target="InvertDiagBlocksLowerTriangular" | custom-call | tf_op jit(solution)/shard_map/triangular_solve | solution.py:34
  74.6 77.7 %all-reduce.2.cloned.1.call-done = f32[4,768,8]{1,2,0:T(8,128)} async-done(((f32[4,768,8]{1,2,0:T(8,128)}), f32[4,768,8]{1,2,0:T(8,128)}) %all-reduce.2.cloned.1.call-update) | async-done | bytes 98320 | tf_op jit(solution)/shard_map/psum | solution.py:24
  152.3 1.0 multiply_reduce_fusion
  153.3 1.1 fusion.9
  154.4 0.2 fusion.12
  154.5 0.0 copy-start.1
  154.5 4.4 %multiply_subtract_fusion = (f32[4,384,192]{1,2,0:T(8,128)}, f32[4,384,192]{1,2,0:T(8,128)}) fusion(f32[4,384,192]{1,2,0:T(8,128)} %param.6, f32[4,384,8]{1,2,0:T(8,128)S(1)} %psum.21, f32[4,8,192]{2,1,0:T(8,128)S(1)} %fusion.12, f32[4,384,192]{1,2,0:T(8,128)} %param.7), kind=kOutput, calls=%fused_computation.7 | convolution fusion | flops 29786112 | bytes 4792320 | tf_op jit(solution)/shard_map/lir,lrw->liw/dot_general | solution.py:35
  158.9 0.0 copy-done.1
  158.9 0.7 broadcast_multiply_fusion
  (7 shorter events, 0.1 us)
Async XLA Ops:
  7.2 1.7 %copy-start = (bf16[1,4,384,768]{3,2,1,0:T(8,128)(2,1)S(1)}, bf16[1,4,384,768]{3,2,1,0:T(8,128)(2,1)}, u32[]{:S(2)}) copy-start(bf16[1,4,384,768]{3,2,1,0:T(8,128)(2,1)} %param.4) | copy-start | bytes 7077892
  7.2 145.1 %all-reduce.2.cloned.1.call-start = ((), (), s32[]{:S(2)}) async-start(), calls=%async_computation | async-start | bytes 196608 | tf_op jit(solution)/shard_map/psum | solution.py:24
  154.5 4.4 %copy-start.1 = (f32[4,768,8]{1,2,0:T(8,128)S(1)}, f32[4,768,8]{1,2,0:T(8,128)}, u32[]{:S(2)}) copy-start(f32[4,768,8]{1,2,0:T(8,128)} %all-reduce.2.cloned.1.call-done) | copy-start | bytes 294916
Sparse Core Ops, SparseCore 0:
  28.3 123.8 all-reduce.1
where the time goes:
time: 167 us; the launch traced here: 166 us
  waiting for transfers between devices  77.7 us (47%)
  blocking collectives  56.2 us (34%)
  between operations  14.1 us (8%)
  matrix products  8.45 us (5%)
  other arithmetic  7.59 us (5%)
  local copies, waits for them, and re-layouts  2.47 us (1%)
    psum x1, waiting for transfers between devices, on_device(): right, gram = lax.psum((part_right, own_share), ('dp', 'tp'))  77.7 us
    psum x1, blocking collectives, on_device(): right, gram = lax.psum((part_right, own_share), ('dp', 'tp'))  39.5 us
    psum x1, blocking collectives, on_device(): left = lax.psum(part_left, 'dp')  16.7 us
    dot_general x1, matrix products, on_device(): jnp.einsum('lir,lrw->liw', left, mixed, precision=lax.Precision.HIGHEST)  4.38 us
  transfers between devices with their start and end apart: 1, of which 1 were waited for; matrix products, arithmetic and copies ran while one was open for 4% of the time, Pallas kernels for 0%

commit v1 on v0

--- a/solution.py
+++ b/solution.py
@@ -21,7 +21,7 @@
         "liw,lir->lwr", own_grads, small_left, preferred_element_type=jnp.float32
     )
     own_share = part_gram / lax.axis_size("dp")
-    right, gram = lax.psum((part_right, own_share), ("dp", "tp"))
+    right, gram = lax.psum(lax.psum((part_right, own_share), "dp"), "tp")
     gram = gram + 0.001 * jnp.mean(jnp.diagonal(gram, axis1=1, axis2=2), axis=1)[
         :, None, None
     ] * jnp.eye(RANK, dtype=jnp.float32)

time: 167 us -> 141 us (0.84)
  waiting for transfers between devices: 77.7 us -> 54.7 us
  blocking collectives: 56.2 us -> 53 us
    psum x1 -> x2, waiting for transfers between devices: 77.7 us -> 54.7 us  [on_device(): right, gram = lax.psum(lax.psum((part_right, own_share), 'dp'), 'tp')]
    psum x1 -> x2, blocking collectives: 39.5 us -> 36.3 us  [on_device(): right, gram = lax.psum(lax.psum((part_right, own_share), 'dp'), 'tp')]
  transfers between devices with their start and end apart: 1 -> 2, of which waited for: 1 -> 2; matrix products, arithmetic and copies ran while one was open for 4% -> 5% of each run, Pallas kernels for 0% -> 0%
where the time goes in v1:
time: 141 us; the launch traced here: 140 us
  waiting for transfers between devices  54.7 us (39%)
  blocking collectives  53 us (38%)
  between operations  14.1 us (10%)
  matrix products  8.45 us (6%)
  other arithmetic  7.6 us (5%)
  local copies, waits for them, and re-layouts  2.46 us (2%)
    psum x2, waiting for transfers between devices, on_device(): right, gram = lax.psum(lax.psum((part_right, own_share), 'dp'), 'tp')  54.7 us
    psum x2, blocking collectives, on_device(): right, gram = lax.psum(lax.psum((part_right, own_share), 'dp'), 'tp')  36.3 us
    psum x1, blocking collectives, on_device(): left = lax.psum(part_left, 'dp')  16.7 us
    dot_general x1, matrix products, on_device(): jnp.einsum('lir,lrw->liw', left, mixed, precision=lax.Precision.HIGHEST)  4.38 us
    another operation x4, other arithmetic, on_device(): root = jnp.linalg.cholesky(gram)  3.09 us
  transfers between devices with their start and end apart: 2, of which 2 were waited for; matrix products, arithmetic and copies ran while one was open for 5% of the time, Pallas kernels for 0%

profile of v1, /device:TPU:8, one launch (start us, length us, event | category | flops | bytes accessed | tf_op | source)
XLA Modules:
  0.0 140.3 jit_solution(3946585352125908093)
XLA Ops:
  7.2 0.0 copy-start
  7.2 0.0 all-reduce.3.cloned.1.call-start
  7.2 1.6 %copy-done = bf16[1,4,384,768]{3,2,1,0:T(8,128)(2,1)S(1)} copy-done((bf16[1,4,384,768]{3,2,1,0:T(8,128)(2,1)S(1)}, bf16[1,4,384,768]{3,2,1,0:T(8,128)(2,1)}, u32[]{:S(2)}) %copy-start) | copy-done | bytes 2359320
  8.8 1.6 %fusion.2 = f32[4,384,8]{1,2,0:T(8,128)S(1)} fusion(bf16[1,4,384,768]{3,2,1,0:T(8,128)(2,1)S(1)} %copy-done, f32[4,768,8]{1,2,0:T(8,128)} %param.5), kind=kOutput, calls=%fused_computation.3 | convolution fusion | flops 18898944 | bytes 2506752 | tf_op jit(solution)/shard_map/liw,lwr->lir/dot_general | solution.py:11
  10.4 16.7 %psum.35 = f32[4,384,8]{1,2,0:T(8,128)S(1)} all-reduce(f32[4,384,8]{1,2,0:T(8,128)S(1)} %fusion.2), channel_id=1, replica_groups=mesh['dp'=4,'tp'=8] {'dp'}, use_global_device_ids=true, to_apply=%region_0.0 | all-reduce | flops 12288 | bytes 98304 | tf_op jit(solution)/shard_map/psum | solution.py:17
  27.1 1.1 fusion.5
  28.2 0.0 all-reduce.3.cloned.1.call-update
  28.2 0.0 all-reduce.5.cloned.1.call-start
  28.3 0.2 convolution_multiply_fusion.1
  28.5 0.1 copy.13
  28.6 13.9 %psum.36 = f32[4,8,8]{1,2,0:T(8,128)S(1)} all-reduce(f32[4,8,8]{1,2,0:T(8,128)S(1)} %convolution_multiply_fusion.1), channel_id=1, replica_groups=mesh['dp'=4,'tp'=8] {'dp'}, use_global_device_ids=true, to_apply=%region_1.0 | all-reduce | flops 256 | bytes 2048 | tf_op jit(solution)/shard_map/psum | solution.py:24
  42.5 22.4 %psum.37 = f32[4,8,8]{1,2,0:T(8,128)S(1)} all-reduce(f32[4,8,8]{1,2,0:T(8,128)S(1)} %psum.36), channel_id=1, replica_groups=mesh['dp'=4,'tp'=8] {'tp'}, use_global_device_ids=true, to_apply=%region_2.0 | all-reduce | flops 256 | bytes 2048 | tf_op jit(solution)/shard_map/psum | solution.py:24
  64.8 0.1 copy.12
  65.0 0.6 gather_fusion
  65.6 0.1 multiply_add_fusion
  65.6 0.1 copy.14
  65.7 0.1 fusion.15
  65.8 2.9 %custom-call.9 = f32[4,8,8]{2,1,0:T(8,128)S(1)} custom-call(f32[4,8,8]{2,1,0:T(8,128)S(1)} %fusion.15), custom_call_target="Cholesky" | custom-call | tf_op jit(solution)/shard_map/jit(cholesky)/cholesky | solution.py:30
  68.7 0.1 select_reduce_fusion
  68.8 0.1 compare_reduce_fusion
  68.9 0.9 all-reduce.3.cloned.1.call-done
  69.8 0.0 all-reduce.5.cloned.1.call-update
  69.8 0.1 select_bitcast_fusion
  69.9 2.5 %custom-call.10 = f32[4,1,8,8]{2,3,1,0:T(8,128)S(1)} custom-call(f32[4,1,8,8]{3,2,1,0:T(8,128)S(1)} %select_bitcast_fusion), custom_call_target="InvertDiagBlocksLowerTriangular" | custom-call | tf_op jit(solution)/shard_map/triangular_solve | solution.py:34
  72.4 53.8 %all-reduce.5.cloned.1.call-done = f32[4,768,8]{1,2,0:T(8,128)} async-done(((f32[4,768,8]{1,2,0:T(8,128)}), f32[4,768,8]{1,2,0:T(8,128)}) %all-reduce.5.cloned.1.call-update) | async-done | bytes 98320 | tf_op jit(solution)/shard_map/psum | solution.py:24
  126.1 1.0 multiply_reduce_fusion
  127.2 1.1 fusion.9
  128.2 0.2 fusion.12
  128.4 0.0 copy-start.1
  128.4 4.4 %multiply_subtract_fusion = (f32[4,384,192]{1,2,0:T(8,128)}, f32[4,384,192]{1,2,0:T(8,128)}) fusion(f32[4,384,192]{1,2,0:T(8,128)} %param.6, f32[4,384,8]{1,2,0:T(8,128)S(1)} %psum.35, f32[4,8,192]{2,1,0:T(8,128)S(1)} %fusion.12, f32[4,384,192]{1,2,0:T(8,128)} %param.7), kind=kOutput, calls=%fused_computation.7 | convolution fusion | flops 29786112 | bytes 4792320 | tf_op jit(solution)/shard_map/lir,lrw->liw/dot_general | solution.py:35
  132.8 0.0 copy-done.1
  132.8 0.7 broadcast_multiply_fusion
  (7 shorter events, 0.1 us)
Async XLA Ops:
  7.2 1.7 %copy-start = (bf16[1,4,384,768]{3,2,1,0:T(8,128)(2,1)S(1)}, bf16[1,4,384,768]{3,2,1,0:T(8,128)(2,1)}, u32[]{:S(2)}) copy-start(bf16[1,4,384,768]{3,2,1,0:T(8,128)(2,1)} %param.4) | copy-start | bytes 7077892
  7.2 62.6 %all-reduce.3.cloned.1.call-start = ((), (), s32[]{:S(2)}) async-start(), calls=%async_computation | async-start | bytes 196608 | tf_op jit(solution)/shard_map/psum | solution.py:24
  28.2 97.9 %all-reduce.5.cloned.1.call-start = ((), (), s32[]{:S(2)}) async-start(), calls=%async_computation.1 | async-start | bytes 196608 | tf_op jit(solution)/shard_map/psum | solution.py:24
  128.4 4.4 %copy-start.1 = (f32[4,768,8]{1,2,0:T(8,128)S(1)}, f32[4,768,8]{1,2,0:T(8,128)}, u32[]{:S(2)}) copy-start(f32[4,768,8]{1,2,0:T(8,128)} %all-reduce.5.cloned.1.call-done) | copy-start | bytes 294916
Sparse Core Ops, SparseCore 0:
  28.3 41.3 all-reduce.2
  72.1 54.0 all-reduce.4

commit v2 on v0

--- a/solution.py
+++ b/solution.py
@@ -14,7 +14,9 @@
         right_factor.astype(jnp.bfloat16),
         preferred_element_type=jnp.float32,
     )
-    left = lax.psum(part_left, "dp")
+    left = part_left
+    for hop in (1, 2):
+        left = left + lax.ppermute(left, "dp", [(dev, dev ^ hop) for dev in range(4)])
     part_gram = jnp.einsum("lir,lis->lrs", left, left, precision=lax.Precision.HIGHEST)
     small_left = left.astype(jnp.bfloat16)
     part_right = jnp.einsum(

time: 167 us -> 204 us (1.22)
  waiting for transfers between devices: 77.7 us -> 127 us
  blocking collectives: 56.2 us -> 40.5 us
  starting transfers between devices: 0.04 us -> 3.11 us
    psum x1, waiting for transfers between devices: 77.7 us -> 122 us  [on_device(): right, gram = lax.psum((part_right, own_share), ('dp', 'tp'))]
    psum x1 -> x0, blocking collectives: 16.7 us -> none  [on_device(): left = lax.psum(part_left, 'dp')]
    ppermute x0 -> x2, waiting for transfers between devices: none -> 5.07 us  [on_device(): lax.ppermute(left, 'dp', [(dev, dev ^ hop) for dev in range(4)])]
    ppermute x0 -> x2, starting transfers between devices: none -> 3.08 us  [on_device(): lax.ppermute(left, 'dp', [(dev, dev ^ hop) for dev in range(4)])]
  transfers between devices with their start and end apart: 1 -> 3, of which waited for: 1 -> 3; matrix products, arithmetic and copies ran while one was open for 4% -> 1% of each run, Pallas kernels for 0% -> 0%
where the time goes in v2:
time: 204 us; the launch traced here: 203 us
  waiting for transfers between devices  127 us (62%)
  blocking collectives  40.5 us (20%)
  between operations  14.1 us (7%)
  matrix products  8.46 us (4%)
  other arithmetic  7.6 us (4%)
  starting transfers between devices  3.11 us (2%)
  local copies, waits for them, and re-layouts  2.46 us (1%)
    psum x1, waiting for transfers between devices, on_device(): right, gram = lax.psum((part_right, own_share), ('dp', 'tp'))  122 us
    psum x1, blocking collectives, on_device(): right, gram = lax.psum((part_right, own_share), ('dp', 'tp'))  40.5 us
    ppermute x2, waiting for transfers between devices, on_device(): lax.ppermute(left, 'dp', [(dev, dev ^ hop) for dev in range(4)])  5.07 us
    dot_general x1, matrix products, on_device(): jnp.einsum('lir,lrw->liw', left, mixed, precision=lax.Precision.HIGHEST)  4.38 us
  transfers between devices with their start and end apart: 3, of which 3 were waited for; matrix products, arithmetic and copies ran while one was open for 1% of the time, Pallas kernels for 0%

profile of v2, /device:TPU:8, one launch (start us, length us, event | category | flops | bytes accessed | tf_op | source)
XLA Modules:
  0.0 203.2 jit_solution(3978452308150643244)
XLA Ops:
  7.2 0.0 copy-start
  7.2 0.0 all-reduce.2.cloned.1.call-start
  7.2 1.6 copy-done
  8.8 1.6 fusion.2
  10.4 1.5 collective-permute-start
  11.9 2.6 %collective-permute-done = f32[4,384,8]{1,2,0:T(8,128)S(1)} collective-permute-done((f32[4,384,8]{1,2,0:T(8,128)S(1)}, f32[4,384,8]{1,2,0:T(8,128)S(1)}, u32[]{:S(2)}, u32[]{:S(2)}) %collective-permute-start) | collective-permute-done | bytes 49184 | tf_op jit(solution)/shard_map/ppermute | solution.py:19
  14.5 1.6 collective-permute-start.1
  16.1 0.1 copy.13
  16.2 2.5 %collective-permute-done.1 = f32[4,384,8]{1,2,0:T(8,128)S(1)} collective-permute-done((f32[4,384,8]{1,2,0:T(8,128)S(1)}, f32[4,384,8]{1,2,0:T(8,128)S(1)}, u32[]{:S(2)}, u32[]{:S(2)}) %collective-permute-start.1) | collective-permute-done | bytes 49184 | tf_op jit(solution)/shard_map/ppermute | solution.py:19
  18.7 0.2 convolution_multiply_fusion.1
  18.9 1.1 fusion.5
  20.0 40.5 %psum.14 = f32[4,8,8]{1,2,0:T(8,128)S(1)} all-reduce(f32[4,8,8]{1,2,0:T(8,128)S(1)} %convolution_multiply_fusion.1), channel_id=1, replica_groups=mesh['dp'=4,'tp'=8] {'dp','tp'}, use_global_device_ids=true, to_apply=%region_0.0 | all-reduce | flops 256 | bytes 2048 | tf_op jit(solution)/shard_map/psum | solution.py:26
  60.4 0.1 copy.12
  60.6 0.6 gather_fusion
  61.2 0.1 multiply_add_fusion
  61.2 0.1 copy.14
  61.3 0.1 fusion.15
  61.4 2.9 %custom-call.9 = f32[4,8,8]{2,1,0:T(8,128)S(1)} custom-call(f32[4,8,8]{2,1,0:T(8,128)S(1)} %fusion.15), custom_call_target="Cholesky" | custom-call | tf_op jit(solution)/shard_map/jit(cholesky)/cholesky | solution.py:32
  64.3 0.1 select_reduce_fusion
  64.3 0.1 compare_reduce_fusion
  64.5 0.0 all-reduce.2.cloned.1.call-update
  64.5 0.1 select_bitcast_fusion
  64.6 2.5 %custom-call.10 = f32[4,1,8,8]{2,3,1,0:T(8,128)S(1)} custom-call(f32[4,1,8,8]{3,2,1,0:T(8,128)S(1)} %select_bitcast_fusion), custom_call_target="InvertDiagBlocksLowerTriangular" | custom-call | tf_op jit(solution)/shard_map/triangular_solve | solution.py:36
  67.1 121.9 %all-reduce.2.cloned.1.call-done = f32[4,768,8]{1,2,0:T(8,128)} async-done(((f32[4,768,8]{1,2,0:T(8,128)}), f32[4,768,8]{1,2,0:T(8,128)}) %all-reduce.2.cloned.1.call-update) | async-done | bytes 98320 | tf_op jit(solution)/shard_map/psum | solution.py:26
  189.0 1.0 multiply_reduce_fusion
  190.0 1.1 fusion.9
  191.1 0.2 fusion.12
  191.2 0.0 copy-start.1
  191.3 4.4 %multiply_subtract_fusion = (f32[4,384,192]{1,2,0:T(8,128)}, f32[4,384,192]{1,2,0:T(8,128)}) fusion(f32[4,384,192]{1,2,0:T(8,128)} %param.6, f32[4,384,8]{1,2,0:T(8,128)S(1)} %add.45, f32[4,8,192]{2,1,0:T(8,128)S(1)} %fusion.12, f32[4,384,192]{1,2,0:T(8,128)} %param.7), kind=kOutput, calls=%fused_computation.7 | convolution fusion | flops 29786112 | bytes 4792320 | tf_op jit(solution)/shard_map/lir,lrw->liw/dot_general | solution.py:37
  195.6 0.0 copy-done.1
  195.6 0.7 broadcast_multiply_fusion
  (9 shorter events, 0.1 us)
Async XLA Ops:
  7.2 1.7 copy-start
  7.2 181.8 %all-reduce.2.cloned.1.call-start = ((), (), s32[]{:S(2)}) async-start(), calls=%async_computation | async-start | bytes 196608 | tf_op jit(solution)/shard_map/psum | solution.py:26
  10.4 4.1 %collective-permute-start = (f32[4,384,8]{1,2,0:T(8,128)S(1)}, f32[4,384,8]{1,2,0:T(8,128)S(1)}, u32[]{:S(2)}, u32[]{:S(2)}) collective-permute-start(f32[4,384,8]{1,2,0:T(8,128)S(1)} %fusion.2), channel_id=1, source_target_pairs={{0,8},{8,0},{16,24},{24,16},{1,9},{9,1},{17,25},{25,17},{2,10},{10... | collective-permute-start | bytes 147464 | tf_op jit(solution)/shard_map/ppermute | solution.py:19
  14.5 4.2 %collective-permute-start.1 = (f32[4,384,8]{1,2,0:T(8,128)S(1)}, f32[4,384,8]{1,2,0:T(8,128)S(1)}, u32[]{:S(2)}, u32[]{:S(2)}) collective-permute-start(f32[4,384,8]{1,2,0:T(8,128)S(1)} %add.44), channel_id=1, source_target_pairs={{0,16},{8,24},{16,0},{24,8},{1,17},{9,25},{17,1},{25,9},{2,18},{10... | collective-permute-start | bytes 147464 | tf_op jit(solution)/shard_map/ppermute | solution.py:19
  191.2 4.4 %copy-start.1 = (f32[4,768,8]{1,2,0:T(8,128)S(1)}, f32[4,768,8]{1,2,0:T(8,128)}, u32[]{:S(2)}) copy-start(f32[4,768,8]{1,2,0:T(8,128)} %all-reduce.2.cloned.1.call-done) | copy-start | bytes 294916
Sparse Core Ops, SparseCore 0:
  64.6 124.3 all-reduce.1
